TPU v7x, 32 devices: a whole 2x2x4 slice. The times are simulated.
32 devices in a mesh: panel: 4 (over x, core), tile: 8 (over z, y).
Axes of the slice: x: 2, y: 2, z: 4, core: 2. Of those that a mesh axis runs over, the one named last changes fastest.
Arguments:
- residual: float32 [4, 8, 16, 8, 128], P('panel', 'tile'), may hold values from -6 to 6
- inverse: bfloat16 [4, 8, 2, 576, 576], P('panel', 'tile'), may hold values from -1 to 2
- blend_weight: float32 [576], replicated, may hold values from 0.1 to 1.9
- seam_table: int32 [4, 4, 3], replicated, may hold values from -1 to 3, as said below
Outputs:
- correction: float32 [4, 8, 16, 8, 128], P('panel', 'tile')
Inputs may be any that keep to these rules, and one draw needn't show every extreme that they name: seam_table[p, e] holds the neighbour panel across edge e of panel p (or -1), a rotation r and a reversal v. Every panel has neighbours across exactly two opposite edges (0 and 2, or 1 and 3) and the entries -1, 0, 0 on the other two; the panels form one closed cycle and each panel's two neighbours differ. If edge e of p faces panel q, then edge c = (e + 2 + r) mod 4 of q faces p with rotation (-r) mod 4 and the same reversal v. At least one seam joins edge 0 of a panel to edge 0 of another, with rotation 2 and reversal 1.
All inputs are finite; a program needn't handle non-finite values.
Results may differ from a plain program's by a relative error of at most 0.0029.
Values may be sent and summed in bfloat16 or wider, within the bound.
A program may use at most 128 MiB of HBM per device.

v0:
```python
import jax
import jax.numpy as jnp
from jax import lax
from jax.sharding import PartitionSpec as P

PANELS = 4
TILE_ROWS = 2
SUB = 8
INTERSECTION = 8


def passed_along(block, axis, distance):
    devices = range(lax.axis_size(axis))
    route = [(i - distance, i) for i in devices if i - distance in devices]
    return lax.ppermute(block, axis, route)


def neighbours_in(first_part, second_part, stride):
    from_below = passed_along(first_part, "tile", stride)
    from_above = passed_along(second_part, "tile", -stride)
    return (from_below, from_above)


def neighbours_out(first_part, second_part, stride):
    to_above = passed_along(first_part, "tile", stride)
    to_below = passed_along(second_part, "tile", -stride)
    return (to_above, to_below)


def band_index(edge_id, row_count, col_count):
    margin = INTERSECTION
    if edge_id == 0:
        return (slice(None), slice(0, margin))
    if edge_id == 1:
        return (slice(0, margin), slice(None))
    if edge_id == 2:
        return (slice(None), slice(col_count - margin, col_count))
    return (slice(row_count - margin, row_count), slice(None))


def to_band(window, edge_id):
    if edge_id == 0:
        return jnp.transpose(window[::-1], (1, 0, 2))
    if edge_id == 1:
        return window[::-1]
    if edge_id == 2:
        return jnp.transpose(window, (1, 0, 2))
    return window


def from_band(region, edge_id):
    if edge_id == 0:
        return jnp.transpose(region, (1, 0, 2))[::-1]
    if edge_id == 1:
        return region[::-1]
    if edge_id == 2:
        return jnp.transpose(region, (1, 0, 2))
    return region


def into_cells(edge_part, edge_id):
    if edge_id == 0:
        return jnp.transpose(edge_part, (1, 0, 2))
    if edge_id == 1:
        return edge_part
    if edge_id == 2:
        return jnp.transpose(edge_part[::-1], (1, 0, 2))
    return edge_part[::-1]


def placed(band, offset, live_edge, length_all):
    blank_band = jnp.zeros((band.shape[0], length_all, band.shape[2]), jnp.float32)
    filled = lax.dynamic_update_slice_in_dim(blank_band, band, offset, 1)
    return jnp.where(live_edge, filled, jnp.zeros_like(filled))


def build_buffer(bands, offsets, live_edge, panel_side, extra):
    length_all = panel_side + 2 * extra
    return jnp.stack(
        [
            (
                placed(bands[2 * slot_id], offsets[2 * slot_id], live_edge[2 * slot_id], length_all)
                + placed(
                    bands[2 * slot_id + 1],
                    offsets[2 * slot_id + 1],
                    live_edge[2 * slot_id + 1],
                    length_all,
                )
            )[:, extra : extra + panel_side]
            for slot_id in range(2)
        ]
    )


def slot_info(seam_row, slot_id):
    first_entry = seam_row[2 * slot_id]
    second_entry = seam_row[2 * slot_id + 1]
    first_live = first_entry[0] >= 0
    chosen = jnp.where(first_live, first_entry, second_entry)
    edge_id = jnp.where(first_live, 2 * slot_id, 2 * slot_id + 1)
    facing = (edge_id + 2 + chosen[1]) % 4
    return (jnp.maximum(chosen[0], 0), facing // 2, chosen[2])


def outgoing_of(totals, slot_facts):
    blank_slot = jnp.zeros_like(totals[0])
    return jnp.stack(
        [
            jnp.where(
                slot_facts[0][0] == target,
                totals[0],
                jnp.where(slot_facts[1][0] == target, totals[1], blank_slot),
            )
            for target in range(PANELS)
        ]
    )


def picked_of(arrived_all, slot_facts):
    return jnp.stack(
        [
            lax.dynamic_index_in_dim(arrived_all, slot_facts[slot_id][0], 0, keepdims=False)
            for slot_id in range(2)
        ]
    )


def gathered_edges(bands, seam_row, tile_rows, tile_cols):
    height = bands[0].shape[1]
    width = bands[1].shape[1]
    longest = max(height, width)
    columns = bands[0].shape[2]
    pieces = []
    for slot_id in range(2):
        column_type = seam_row[2 * slot_id, 0] >= 0
        column_band = bands[2 * slot_id]
        row_band = jnp.pad(bands[2 * slot_id + 1], ((0, 0), (0, longest - width), (0, 0)))
        pieces.append(jnp.where(column_type, column_band, row_band))
    gathered = lax.all_gather(jnp.stack(pieces)[None], "tile", axis=0, tiled=True)
    grid = gathered.reshape(tile_rows, tile_cols, 2, INTERSECTION, longest, columns)
    totals = []
    for slot_id in range(2):
        column_type = seam_row[2 * slot_id, 0] >= 0
        grid_col = 0 if slot_id == 0 else tile_cols - 1
        grid_row = 0 if slot_id == 0 else tile_rows - 1
        down_column = grid[:, grid_col, slot_id, :, :height]
        down_column = jnp.transpose(down_column, (1, 0, 2, 3)).reshape(
            INTERSECTION, tile_rows * height, columns
        )
        along_row = grid[grid_row, :, slot_id, :, :width]
        along_row = jnp.transpose(along_row, (1, 0, 2, 3)).reshape(
            INTERSECTION, tile_cols * width, columns
        )
        totals.append(jnp.where(column_type, down_column, along_row))
    return jnp.stack(totals)


def cross(bands, seam_row, forward, offsets, live_edge, panel_side, tile_rows, tile_cols):
    extra = 0 if forward else INTERSECTION
    slot_facts = [slot_info(seam_row, slot_id) for slot_id in range(2)]
    if forward:
        totals = gathered_edges(bands, seam_row, tile_rows, tile_cols)
        arrived_all = lax.all_to_all(
            outgoing_of(totals, slot_facts), "panel", split_axis=0, concat_axis=0, tiled=True
        )
    else:
        buffer = build_buffer(bands, offsets, live_edge, panel_side, extra)
        totals = lax.psum(buffer, "tile")
        arrived_all = lax.all_to_all(
            outgoing_of(totals, slot_facts), "panel", split_axis=0, concat_axis=0, tiled=True
        )
    arrived = picked_of(arrived_all, slot_facts)
    return [
        jnp.where(slot_facts[slot_id][2] > 0, arrived[slot_id][:, ::-1], arrived[slot_id])
        for slot_id in range(2)
    ]


def patches(padded, block_rows, block_cols):
    columns = padded.shape[-1]
    blocked = padded.reshape(block_rows + 2, SUB, block_cols + 2, SUB, columns)
    pieces = [
        blocked[row_shift : row_shift + block_rows, :, col_shift : col_shift + block_cols]
        for row_shift in range(3)
        for col_shift in range(3)
    ]
    stacked = jnp.stack(pieces).reshape(3, 3, block_rows, SUB, block_cols, SUB, columns)
    stacked = jnp.transpose(stacked, (2, 4, 0, 3, 1, 5, 6))
    return stacked.reshape(block_rows, block_cols, 9 * SUB * SUB, columns)


def intersection_add(solved, block_rows, block_cols):
    columns = solved.shape[-1]
    shaped = solved.reshape(block_rows, block_cols, 3, SUB, 3, SUB, columns)
    summed = jnp.zeros((block_rows + 2, SUB, block_cols + 2, SUB, columns), jnp.float32)
    for row_shift in range(3):
        for col_shift in range(3):
            block_part = jnp.transpose(shaped[:, :, row_shift, :, col_shift], (0, 2, 1, 3, 4))
            summed = summed.at[
                row_shift : row_shift + block_rows, :, col_shift : col_shift + block_cols
            ].add(block_part)
    return summed.reshape((block_rows + 2) * SUB, (block_cols + 2) * SUB, columns)


def local(residual, inverse, blend_weight, seam_table):
    margin = INTERSECTION
    source = residual[0, 0].astype(jnp.bfloat16)
    height, tile_width, columns = source.shape
    tile_rows = TILE_ROWS
    tile_cols = lax.axis_size("tile") // TILE_ROWS
    tile_id = lax.axis_index("tile")
    row_pos = tile_id // tile_cols
    col_pos = tile_id % tile_cols
    seam_row = lax.dynamic_index_in_dim(seam_table, lax.axis_index("panel"), 0, keepdims=False)
    panel_side = tile_width * tile_cols
    on_edge = [col_pos == 0, row_pos == 0, col_pos == tile_cols - 1, row_pos == tile_rows - 1]
    live_edge = [on_edge[edge_id] & (seam_row[edge_id, 0] >= 0) for edge_id in range(4)]
    offsets = [row_pos * height, col_pos * tile_width, row_pos * height, col_pos * tile_width]
    lengths = [height, tile_width, height, tile_width]
    left_valid = col_pos > 0
    right_valid = col_pos < tile_cols - 1
    below_rows, above_rows = neighbours_in(source[height - margin :], source[:margin], tile_cols)
    row_ext = jnp.concatenate([below_rows, source, above_rows], 0)
    left_cols, right_cols = neighbours_in(row_ext, row_ext, 1)
    left_cols = jnp.where(left_valid, left_cols, jnp.zeros_like(left_cols))
    right_cols = jnp.where(right_valid, right_cols, jnp.zeros_like(right_cols))
    extended = jnp.concatenate([left_cols, row_ext, right_cols], 1)
    own_strips = [
        jnp.transpose(source, (1, 0, 2)),
        source[:margin],
        jnp.transpose(source[:, ::-1], (1, 0, 2)),
        source[height - margin :][::-1],
    ]
    arrived = cross(
        own_strips, seam_row, True, offsets, live_edge, panel_side, tile_rows, tile_cols
    )
    rows_ext, cols_ext = (extended.shape[0], extended.shape[1])
    for edge_id in range(4):
        widened = jnp.pad(arrived[edge_id // 2], ((0, 0), (margin, margin), (0, 0)))
        window = lax.dynamic_slice_in_dim(
            widened, offsets[edge_id], lengths[edge_id] + 2 * margin, 1
        )
        where_band = band_index(edge_id, rows_ext, cols_ext)
        fresh_band = jnp.where(live_edge[edge_id], to_band(window, edge_id), extended[where_band])
        extended = extended.at[where_band].set(fresh_band)
    sub_rows, sub_cols = (height // SUB, tile_width // SUB)
    local_patches = patches(extended, sub_rows, sub_cols).reshape(
        sub_rows * sub_cols, 9 * SUB * SUB, columns
    )
    solved = jnp.einsum(
        "noi,nir->nor", inverse[0, 0], local_patches, preferred_element_type=jnp.float32
    )
    solved = solved * blend_weight[None, :, None]
    spread = intersection_add(
        solved.reshape(sub_rows, sub_cols, 9 * SUB * SUB, columns), sub_rows, sub_cols
    )
    ghost_sets = [
        from_band(spread[band_index(edge_id, rows_ext, cols_ext)], edge_id) for edge_id in range(4)
    ]
    returned = cross(
        ghost_sets, seam_row, False, offsets, live_edge, panel_side, tile_rows, tile_cols
    )
    got_left, got_right = neighbours_out(spread[:, tile_width + margin :], spread[:, :margin], 1)
    spread = spread.at[:, margin : 2 * margin].add(jnp.where(left_valid, got_left, 0.0))
    spread = spread.at[:, tile_width : tile_width + margin].add(
        jnp.where(right_valid, got_right, 0.0)
    )
    narrow = spread[:, margin : tile_width + margin]
    got_below, got_above = neighbours_out(narrow[height + margin :], narrow[:margin], tile_cols)
    narrow = narrow.at[margin : 2 * margin].add(got_below)
    narrow = narrow.at[height : height + margin].add(got_above)
    owned_cells = narrow[margin : height + margin]
    for edge_id in range(4):
        edge_part = lax.dynamic_slice_in_dim(
            returned[edge_id // 2], offsets[edge_id], lengths[edge_id], 1
        )
        where_cells = band_index(edge_id, height, tile_width)
        addition = jnp.where(live_edge[edge_id], into_cells(edge_part, edge_id), 0.0)
        owned_cells = owned_cells.at[where_cells].add(addition)
    return owned_cells[None, None]


def solution(mesh):
    placed = (P("panel", "tile", None, None, None), P("panel", "tile", None, None, None), P(), P())
    return jax.shard_map(
        local,
        mesh=mesh,
        in_specs=placed,
        out_specs=P("panel", "tile", None, None, None),
        check_vma=False,
    )
```

profile of v0, /device:TPU:0, one launch (start us, length us, event | category | flops | bytes accessed | tf_op | source)
XLA Modules:
  0.0 179.4 jit_solution(4141283619340578663)
XLA Ops:
  6.5 1.0 convert_element_type.14
  7.5 1.3 collective-permute-start.1
  8.8 6.0 %collective-permute-start = (bf16[8,8,128]{2,1,0:T(8,128)(2,1)S(1)}, bf16[8,8,128]{2,1,0:T(8,128)(2,1)S(1)}, u32[]{:S(2)}, u32[]{:S(2)}) collective-permute-start(bf16[8,8,128]{2,1,0:T(8,128)(2,1)S(1)} %get-tuple-element.301), channel_id=1, source_target_pairs={{0,4},{1,5},{2,6},{3,7},{8,12},{9,13},{10,14},{11,15},{16,20},{17,... | collective-permute-start | bytes 49160 | tf_op jit(solution)/shard_map/ppermute | solution.py:15
  14.8 0.8 convert_bitcast_fusion.1
  15.6 0.8 convert_bitcast_fusion
  16.5 0.7 constant_dynamic-slice_fusion.8
  17.2 0.1 copy.95
  17.3 0.6 fusion.51
  19.3 31.4 %all-gather = bf16[16,8,16,128]{3,2,1,0:T(8,128)(2,1)S(1)} all-gather(bf16[2,8,16,128]{3,2,1,0:T(8,128)(2,1)S(1)} %pad_maximum_fusion.5), channel_id=2, replica_groups=mesh['panel'=4,'tile'=8] {'tile'}, dimensions={0}, use_global_device_ids=true | all-gather | bytes 589824 | tf_op jit(solution)/shard_map/all_gather | solution.py:139
  50.8 0.7 constant_dynamic-slice_fusion.1
  52.8 0.1 broadcast_select_fusion.8
  52.8 0.6 fusion.52
  54.7 0.7 pad_maximum_fusion.1
  55.5 3.6 %all-to-all-start = ((bf16[4,8,32,128]{3,2,1,0:T(8,128)(2,1)}), bf16[4,8,32,128]{3,2,1,0:T(8,128)(2,1)S(1)}, u32[]{:S(2)}, u32[]{:S(2)}) async-start(bf16[4,8,32,128]{3,2,1,0:T(8,128)(2,1)} %pad_maximum_fusion.1), calls=%async_computation | async-start | bytes 524288 | tf_op jit(solution)/shard_map/all_to_all | solution.py:163
  59.1 0.6 fusion.54
  62.3 0.6 slice.865
  62.9 1.3 concatenate.55
  64.2 0.8 concatenate.54
  65.0 0.0 collective-permute-done.1
  65.0 0.0 collective-permute-done
  65.0 1.3 collective-permute-start.3
  66.3 0.6 and_reduce_fusion
  66.9 4.5 %collective-permute-start.2 = (bf16[32,8,128]{2,1,0:T(8,128)(2,1)S(1)}, bf16[32,8,128]{2,1,0:T(8,128)(2,1)S(1)}, u32[]{:S(2)}, u32[]{:S(2)}) collective-permute-start(bf16[32,8,128]{2,1,0:T(8,128)(2,1)S(1)} %pad_maximum_fusion.4), channel_id=1, source_target_pairs={{0,1},{1,2},{2,3},{3,4},{4,5},{5,6},{6,7},{8,9},{9,10},{10,11},{11... | collective-permute-start | bytes 196616 | tf_op jit(solution)/shard_map/ppermute | solution.py:15
  71.5 1.9 %collective-permute-done.2 = bf16[32,8,128]{2,1,0:T(8,128)(2,1)S(1)} collective-permute-done((bf16[32,8,128]{2,1,0:T(8,128)(2,1)S(1)}, bf16[32,8,128]{2,1,0:T(8,128)(2,1)S(1)}, u32[]{:S(2)}, u32[]{:S(2)}) %collective-permute-start.2) | collective-permute-done | bytes 65568 | tf_op jit(solution)/shard_map/ppermute | solution.py:15
  73.4 0.0 all-to-all-done
  73.5 0.0 copy-start.2
  73.7 0.1 fusion.25
  74.0 0.1 copy.112
  74.1 0.1 copy-done.2
  74.2 0.5 fusion.2
  74.8 1.3 fusion.7
  76.1 1.8 %fusion.8 = f32[4,8,3,8,128]{4,3,1,0,2:T(8,128)S(1)} fusion(f32[4,8,3,8,128]{4,3,1,0,2:T(8,128)S(1)} %fusion.7, s32[]{:T(128)} %bitcast.56, s32[]{:T(128)} %bitcast.57, f32[2,1,3,8,3,8,128]{6,5,4,3,2,0,1:T(8,128)S(1)} %bitcast.226, pred[]{:T(512)} %get-tuple-element.273), kind=kLoop, calls=%fused_computation.33 | loop fusion | flops 32768 | bytes 196617 | tf_op jit(solution)/shard_map/scatter-add | solution.py:201
  78.2 1.3 collective-permute-start.5
  79.5 4.9 %collective-permute-start.4 = (f32[32,8,128]{2,1,0:T(8,128)S(1)}, f32[32,8,128]{2,1,0:T(8,128)S(1)}, u32[]{:S(2)}, u32[]{:S(2)}) collective-permute-start(f32[32,8,128]{2,1,0:T(8,128)S(1)} %get-tuple-element.289), channel_id=1, source_target_pairs={{0,1},{1,2},{2,3},{3,4},{4,5},{5,6},{6,7},{8,9},{9,10},{10,11},{11... | collective-permute-start | bytes 393224 | tf_op jit(solution)/shard_map/ppermute | solution.py:15
  84.7 0.7 pad_maximum_fusion.2
  85.4 0.0 all-reduce.7.cloned.1.call-update
  85.4 0.0 collective-permute-done.5
  85.4 2.7 %collective-permute-done.4 = f32[32,8,128]{2,1,0:T(8,128)S(1)} collective-permute-done((f32[32,8,128]{2,1,0:T(8,128)S(1)}, f32[32,8,128]{2,1,0:T(8,128)S(1)}, u32[]{:S(2)}, u32[]{:S(2)}) %collective-permute-start.4) | collective-permute-done | bytes 131104 | tf_op jit(solution)/shard_map/ppermute | solution.py:15
  88.2 4.1 %collective-permute-start.6 = (f32[8,8,128]{2,1,0:T(8,128)S(1)}, f32[8,8,128]{2,1,0:T(8,128)S(1)}, u32[]{:S(2)}, u32[]{:S(2)}) collective-permute-start(f32[8,8,128]{2,1,0:T(8,128)S(1)} %slice.940), channel_id=1, source_target_pairs={{0,4},{1,5},{2,6},{3,7},{8,12},{9,13},{10,14},{11,15},{16,20},{17,... | collective-permute-start | bytes 98312 | tf_op jit(solution)/shard_map/ppermute | solution.py:15
  92.2 64.6 %all-reduce.7.cloned.1.call-done = f32[2,8,32,128]{3,2,1,0:T(8,128)} async-done(((f32[2,8,32,128]{3,2,1,0:T(8,128)}), f32[2,8,32,128]{3,2,1,0:T(8,128)}) %all-reduce.7.cloned.1.call-update) | async-done | bytes 262160 | tf_op jit(solution)/shard_map/psum | solution.py:168
  156.9 1.0 select_select_fusion.3
  157.9 0.9 pad_maximum_fusion
  158.7 3.5 %all-to-all-start.1 = ((f32[4,8,32,128]{3,2,1,0:T(8,128)}), f32[4,8,32,128]{3,2,1,0:T(8,128)S(1)}, u32[]{:S(2)}, u32[]{:S(2)}) async-start(f32[4,8,32,128]{3,2,1,0:T(8,128)} %pad_maximum_fusion), calls=%async_computation.1 | async-start | bytes 1048576 | tf_op jit(solution)/shard_map/all_to_all | solution.py:169
  162.3 1.3 collective-permute-start.7
  163.6 6.0 %collective-permute-done.7 = f32[8,8,128]{2,1,0:T(8,128)S(1)} collective-permute-done((f32[8,8,128]{2,1,0:T(8,128)S(1)}, f32[8,8,128]{2,1,0:T(8,128)S(1)}, u32[]{:S(2)}, u32[]{:S(2)}) %collective-permute-start.7) | collective-permute-done | bytes 32800 | tf_op jit(solution)/shard_map/ppermute | solution.py:15
  169.6 1.4 all-to-all-done.1
  171.3 0.6 copy.201
  171.9 0.6 fusion.30
  (87 shorter events, 1.4 us)
Async XLA Ops:
  6.5 67.5 %copy-start = (bf16[1,1,2,576,576]{4,3,2,1,0:T(8,128)(2,1)S(1)}, bf16[1,1,2,576,576]{4,3,2,1,0:T(8,128)(2,1)}, u32[]{:S(2)}) copy-start(bf16[1,1,2,576,576]{4,3,2,1,0:T(8,128)(2,1)} %param.51) | copy-start | bytes 3981316
  6.5 44.2 %copy-start.1 = (s32[4,4,3]{1,0,2:T(4,128)S(1)}, s32[4,4,3]{1,0,2:T(4,128)}, u32[]{:S(2)}) copy-start(s32[4,4,3]{1,0,2:T(4,128)} %param.53) | copy-start | bytes 580
  7.5 57.4 %collective-permute-start.1 = (bf16[8,8,128]{2,1,0:T(8,128)(2,1)S(1)}, bf16[8,8,128]{2,1,0:T(8,128)(2,1)S(1)}, u32[]{:S(2)}, u32[]{:S(2)}) collective-permute-start(bf16[8,8,128]{2,1,0:T(8,128)(2,1)S(1)} %get-tuple-element.302), channel_id=1, source_target_pairs={{4,0},{5,1},{6,2},{7,3},{12,8},{13,9},{14,10},{15,11},{20,16},{21,... | collective-permute-start | bytes 49160 | tf_op jit(solution)/shard_map/ppermute | solution.py:15
  8.8 56.2 %collective-permute-start = (bf16[8,8,128]{2,1,0:T(8,128)(2,1)S(1)}, bf16[8,8,128]{2,1,0:T(8,128)(2,1)S(1)}, u32[]{:S(2)}, u32[]{:S(2)}) collective-permute-start(bf16[8,8,128]{2,1,0:T(8,128)(2,1)S(1)} %get-tuple-element.301), channel_id=1, source_target_pairs={{0,4},{1,5},{2,6},{3,7},{8,12},{9,13},{10,14},{11,15},{16,20},{17,... | collective-permute-start | bytes 49160 | tf_op jit(solution)/shard_map/ppermute | solution.py:15
  50.7 15.6 %copy-start.3 = (s32[5]{0:T(128)S(1)}, s32[5]{0:T(128)}, u32[]{:S(2)}) copy-start(s32[5]{0:T(128)} %constant.662.clone.1) | copy-start | bytes 64
  55.5 18.0 %all-to-all-start = ((bf16[4,8,32,128]{3,2,1,0:T(8,128)(2,1)}), bf16[4,8,32,128]{3,2,1,0:T(8,128)(2,1)S(1)}, u32[]{:S(2)}, u32[]{:S(2)}) async-start(bf16[4,8,32,128]{3,2,1,0:T(8,128)(2,1)} %pad_maximum_fusion.1), calls=%async_computation | async-start | bytes 524288 | tf_op jit(solution)/shard_map/all_to_all | solution.py:163
  59.1 97.7 %all-reduce.7.cloned.1.call-start = ((), (), s32[]{:S(2)}) async-start(), calls=%async_computation.2 | async-start | bytes 524288 | tf_op jit(solution)/shard_map/psum | solution.py:168
  65.0 6.5 %collective-permute-start.3 = (bf16[32,8,128]{2,1,0:T(8,128)(2,1)S(1)}, bf16[32,8,128]{2,1,0:T(8,128)(2,1)S(1)}, u32[]{:S(2)}, u32[]{:S(2)}) collective-permute-start(bf16[32,8,128]{2,1,0:T(8,128)(2,1)S(1)} %pad_maximum_fusion.4), channel_id=1, source_target_pairs={{1,0},{2,1},{3,2},{4,3},{5,4},{6,5},{7,6},{9,8},{10,9},{11,10},{12... | collective-permute-start | bytes 196616 | tf_op jit(solution)/shard_map/ppermute | solution.py:15
  66.9 6.4 %collective-permute-start.2 = (bf16[32,8,128]{2,1,0:T(8,128)(2,1)S(1)}, bf16[32,8,128]{2,1,0:T(8,128)(2,1)S(1)}, u32[]{:S(2)}, u32[]{:S(2)}) collective-permute-start(bf16[32,8,128]{2,1,0:T(8,128)(2,1)S(1)} %pad_maximum_fusion.4), channel_id=1, source_target_pairs={{0,1},{1,2},{2,3},{3,4},{4,5},{5,6},{6,7},{8,9},{9,10},{10,11},{11... | collective-permute-start | bytes 196616 | tf_op jit(solution)/shard_map/ppermute | solution.py:15
  73.5 0.7 copy-start.2
  78.2 7.2 %collective-permute-start.5 = (f32[32,8,128]{2,1,0:T(8,128)S(1)}, f32[32,8,128]{2,1,0:T(8,128)S(1)}, u32[]{:S(2)}, u32[]{:S(2)}) collective-permute-start(f32[32,8,128]{2,1,0:T(8,128)S(1)} %get-tuple-element.288), channel_id=1, source_target_pairs={{1,0},{2,1},{3,2},{4,3},{5,4},{6,5},{7,6},{9,8},{10,9},{11,10},{12... | collective-permute-start | bytes 393224 | tf_op jit(solution)/shard_map/ppermute | solution.py:15
  79.5 8.7 %collective-permute-start.4 = (f32[32,8,128]{2,1,0:T(8,128)S(1)}, f32[32,8,128]{2,1,0:T(8,128)S(1)}, u32[]{:S(2)}, u32[]{:S(2)}) collective-permute-start(f32[32,8,128]{2,1,0:T(8,128)S(1)} %get-tuple-element.289), channel_id=1, source_target_pairs={{0,1},{1,2},{2,3},{3,4},{4,5},{5,6},{6,7},{8,9},{9,10},{10,11},{11... | collective-permute-start | bytes 393224 | tf_op jit(solution)/shard_map/ppermute | solution.py:15
  88.2 74.1 %collective-permute-start.6 = (f32[8,8,128]{2,1,0:T(8,128)S(1)}, f32[8,8,128]{2,1,0:T(8,128)S(1)}, u32[]{:S(2)}, u32[]{:S(2)}) collective-permute-start(f32[8,8,128]{2,1,0:T(8,128)S(1)} %slice.940), channel_id=1, source_target_pairs={{0,4},{1,5},{2,6},{3,7},{8,12},{9,13},{10,14},{11,15},{16,20},{17,... | collective-permute-start | bytes 98312 | tf_op jit(solution)/shard_map/ppermute | solution.py:15
  158.7 12.3 %all-to-all-start.1 = ((f32[4,8,32,128]{3,2,1,0:T(8,128)}), f32[4,8,32,128]{3,2,1,0:T(8,128)S(1)}, u32[]{:S(2)}, u32[]{:S(2)}) async-start(f32[4,8,32,128]{3,2,1,0:T(8,128)} %pad_maximum_fusion), calls=%async_computation.1 | async-start | bytes 1048576 | tf_op jit(solution)/shard_map/all_to_all | solution.py:169
  162.3 7.3 %collective-permute-start.7 = (f32[8,8,128]{2,1,0:T(8,128)S(1)}, f32[8,8,128]{2,1,0:T(8,128)S(1)}, u32[]{:S(2)}, u32[]{:S(2)}) collective-permute-start(f32[8,8,128]{2,1,0:T(8,128)S(1)} %get-tuple-element.296), channel_id=1, source_target_pairs={{4,0},{5,1},{6,2},{7,3},{12,8},{13,9},{14,10},{15,11},{20,16},{21,... | collective-permute-start | bytes 98312 | tf_op jit(solution)/shard_map/ppermute | solution.py:15
Sparse Core Ops, SparseCore 0:
  85.5 71.2 all-reduce.6
where the time goes:
time: 180 us; the launch traced here: 179 us
  waiting for transfers between devices  76.6 us (43%)
  starting transfers between devices  31.7 us (18%)
  blocking collectives  31.4 us (17%)
  between operations  20.5 us (11%)
  other arithmetic  11.2 us (6%)
  local copies, waits for them, and re-layouts  7.37 us (4%)
    psum x1, waiting for transfers between devices, cross(): totals = lax.psum(buffer, 'tile')  64.6 us
    all_gather x1, blocking collectives, gathered_edges(): lax.all_gather(jnp.stack(pieces)[None], 'tile', axis=0, tiled=True)  31.4 us
    ppermute x8, starting transfers between devices, passed_along(): return lax.ppermute(block, axis, route)  24.6 us
    ppermute x8, waiting for transfers between devices, passed_along(): return lax.ppermute(block, axis, route)  10.6 us
    all_to_all x2, starting transfers between devices, cross(): lax.all_to_all(outgoing_of(totals, slot_facts), 'panel', split_axis=0, co...  7.11 us
  transfers between devices with their start and end apart: 11, of which 5 were waited for; matrix products, arithmetic and copies ran while one was open for 7% of the time, Pallas kernels for 0%

commit v1 on v0

--- a/solution.py
+++ b/solution.py
@@ -165,7 +165,7 @@
         )
     else:
         buffer = build_buffer(bands, offsets, live_edge, panel_side, extra)
-        totals = lax.psum(buffer, "tile")
+        totals = jnp.sum(lax.all_gather(buffer, "tile"), axis=0)
         arrived_all = lax.all_to_all(
             outgoing_of(totals, slot_facts), "panel", split_axis=0, concat_axis=0, tiled=True
         )

time: 180 us -> 151 us (0.84)
  waiting for transfers between devices: 76.6 us -> 51.8 us
  starting transfers between devices: 31.7 us -> 28.3 us
  other arithmetic: 11.2 us -> 8.27 us
  local copies, waits for them, and re-layouts: 7.37 us -> 9.44 us
    psum x1 -> x0, waiting for transfers between devices: 64.6 us -> none  [cross(): totals = lax.psum(buffer, 'tile')]
    all_gather x0 -> x1, waiting for transfers between devices: none -> 35.9 us  [cross(): totals = jnp.sum(lax.all_gather(buffer, 'tile'), axis=0)]
    ppermute x8, starting transfers between devices: 24.6 us -> 21.2 us  [passed_along(): return lax.ppermute(block, axis, route)]
    ppermute x8, waiting for transfers between devices: 10.6 us -> 13.9 us  [passed_along(): return lax.ppermute(block, axis, route)]
    reduce_sum x0 -> x1, other arithmetic: none -> 1.82 us  [cross(): totals = jnp.sum(lax.all_gather(buffer, 'tile'), axis=0)]
    convert_element_type x2 -> x0, other arithmetic: 1.82 us -> none  [local(): source = residual[0, 0].astype(jnp.bfloat16)]
  transfers between devices with their start and end apart: 11 -> 11, of which waited for: 5 -> 6; matrix products, arithmetic and copies ran while one was open for 7% -> 7% of each run, Pallas kernels for 0% -> 0%
where the time goes in v1:
time: 151 us; the launch traced here: 150 us
  waiting for transfers between devices  51.8 us (34%)
  blocking collectives  31.4 us (21%)
  starting transfers between devices  28.3 us (19%)
  between operations  20.6 us (14%)
  local copies, waits for them, and re-layouts  9.44 us (6%)
  other arithmetic  8.27 us (5%)
    all_gather x1, waiting for transfers between devices, cross(): totals = jnp.sum(lax.all_gather(buffer, 'tile'), axis=0)  35.9 us
    all_gather x1, blocking collectives, gathered_edges(): lax.all_gather(jnp.stack(pieces)[None], 'tile', axis=0, tiled=True)  31.4 us
    ppermute x8, starting transfers between devices, passed_along(): return lax.ppermute(block, axis, route)  21.2 us
    ppermute x8, waiting for transfers between devices, passed_along(): return lax.ppermute(block, axis, route)  13.9 us
    all_to_all x2, starting transfers between devices, cross(): lax.all_to_all(outgoing_of(totals, slot_facts), 'panel', split_axis=0, co...  7.11 us
    another operation x8, local copies, waits for them, and re-layouts  3.42 us
    scatter-add x8, other arithmetic, intersection_add(): summed = summed.at[row_shift:row_shift + block_rows, :, col_shift:col_shi...  3.29 us
  transfers between devices with their start and end apart: 11, of which 6 were waited for; matrix products, arithmetic and copies ran while one was open for 7% of the time, Pallas kernels for 0%

profile of v1, /device:TPU:0, one launch (start us, length us, event | category | flops | bytes accessed | tf_op | source)
XLA Modules:
  0.0 150.4 jit_solution(12515410976228673449)
XLA Ops:
  6.5 1.0 copy.315
  7.5 1.3 collective-permute-start.1
  8.8 6.0 %collective-permute-start = (bf16[8,8,128]{2,0,1:T(8,128)(2,1)S(1)}, bf16[8,8,128]{2,0,1:T(8,128)(2,1)S(1)}, u32[]{:S(2)}, u32[]{:S(2)}) collective-permute-start(bf16[8,8,128]{2,0,1:T(8,128)(2,1)S(1)} %get-tuple-element.302), channel_id=1, source_target_pairs={{0,4},{1,5},{2,6},{3,7},{8,12},{9,13},{10,14},{11,15},{16,20},{17,... | collective-permute-start | bytes 49160 | tf_op jit(solution)/shard_map/ppermute | solution.py:15
  14.9 0.7 constant_dynamic-slice_fusion.8
  15.6 0.1 copy.215
  15.7 0.6 fusion.44
  17.6 31.4 %all-gather = bf16[16,8,16,128]{3,2,1,0:T(8,128)(2,1)S(1)} all-gather(bf16[2,8,16,128]{3,2,1,0:T(8,128)(2,1)S(1)} %copy.216), channel_id=2, replica_groups=mesh['panel'=4,'tile'=8] {'tile'}, dimensions={0}, use_global_device_ids=true | all-gather | bytes 589824 | tf_op jit(solution)/shard_map/all_gather | solution.py:139
  49.1 0.0 copy-start.3
  49.1 0.6 constant_dynamic-slice_fusion.2
  51.0 0.1 broadcast_select_fusion.3
  51.1 0.6 fusion.45
  53.1 0.1 select_select_fusion.7
  53.2 0.7 pad_maximum_fusion.1
  53.9 3.6 %all-to-all-start = ((bf16[4,8,32,128]{3,1,2,0:T(8,128)(2,1)}), bf16[4,8,32,128]{3,1,2,0:T(8,128)(2,1)S(1)}, u32[]{:S(2)}, u32[]{:S(2)}) async-start(bf16[4,8,32,128]{3,1,2,0:T(8,128)(2,1)} %pad_maximum_fusion.1), calls=%async_computation | async-start | bytes 524288 | tf_op jit(solution)/shard_map/all_to_all | solution.py:163
  57.6 0.6 fusion.47
  60.7 0.6 slice.865
  61.4 1.3 concatenate.55
  62.7 0.8 concatenate.54
  63.5 1.3 collective-permute-start.3
  64.9 0.6 and_reduce_fusion
  65.5 4.5 %collective-permute-start.2 = (bf16[32,8,128]{2,1,0:T(8,128)(2,1)S(1)}, bf16[32,8,128]{2,1,0:T(8,128)(2,1)S(1)}, u32[]{:S(2)}, u32[]{:S(2)}) collective-permute-start(bf16[32,8,128]{2,1,0:T(8,128)(2,1)S(1)} %pad_maximum_fusion.4), channel_id=1, source_target_pairs={{0,1},{1,2},{2,3},{3,4},{4,5},{5,6},{6,7},{8,9},{9,10},{10,11},{11... | collective-permute-start | bytes 196616 | tf_op jit(solution)/shard_map/ppermute | solution.py:15
  70.0 0.0 collective-permute-done.3
  70.1 1.9 %collective-permute-done.2 = bf16[32,8,128]{2,1,0:T(8,128)(2,1)S(1)} collective-permute-done((bf16[32,8,128]{2,1,0:T(8,128)(2,1)S(1)}, bf16[32,8,128]{2,1,0:T(8,128)(2,1)S(1)}, u32[]{:S(2)}, u32[]{:S(2)}) %collective-permute-start.2) | collective-permute-done | bytes 65568 | tf_op jit(solution)/shard_map/ppermute | solution.py:15
  72.0 0.1 pad_dynamic-slice_fusion.4
  72.1 0.0 copy-start.2
  72.2 0.1 pad_dynamic-slice_fusion.3
  72.7 0.1 copy.238
  72.8 0.0 copy-done.2
  72.8 0.5 fusion.2
  73.4 1.3 fusion.6
  74.7 1.9 %fusion.7 = f32[4,8,3,8,128]{4,3,1,0,2:T(8,128)S(1)} fusion(f32[4,8,3,8,128]{4,3,1,0,2:T(8,128)S(1)} %fusion.6, s32[]{:T(128)} %bitcast.56, s32[]{:T(128)} %bitcast.57, f32[2,1,3,8,3,8,128]{6,5,4,3,2,0,1:T(8,128)S(1)} %bitcast.227, pred[]{:T(512)} %get-tuple-element.273), kind=kLoop, calls=%fused_computation.37 | loop fusion | flops 32768 | bytes 196617 | tf_op jit(solution)/shard_map/scatter-add | solution.py:201
  76.9 0.1 copy_dynamic-update-slice_fusion
  77.3 0.7 copy.256
  78.0 0.0 all-gather.4.cloned.1.call-update
  78.0 4.3 %collective-permute-start.4 = (f32[32,8,128]{2,1,0:T(8,128)S(1)}, f32[32,8,128]{2,1,0:T(8,128)S(1)}, u32[]{:S(2)}, u32[]{:S(2)}) collective-permute-start(f32[32,8,128]{2,1,0:T(8,128)S(1)} %get-tuple-element.288), channel_id=1, source_target_pairs={{0,1},{1,2},{2,3},{3,4},{4,5},{5,6},{6,7},{8,9},{9,10},{10,11},{11... | collective-permute-start | bytes 393224 | tf_op jit(solution)/shard_map/ppermute | solution.py:15
  82.3 1.3 collective-permute-start.5
  83.6 1.2 collective-permute-done.4
  84.8 5.4 %collective-permute-done.5 = f32[32,8,128]{2,1,0:T(8,128)S(1)} collective-permute-done((f32[32,8,128]{2,1,0:T(8,128)S(1)}, f32[32,8,128]{2,1,0:T(8,128)S(1)}, u32[]{:S(2)}, u32[]{:S(2)}) %collective-permute-start.5) | collective-permute-done | bytes 131104 | tf_op jit(solution)/shard_map/ppermute | solution.py:15
  90.3 1.3 collective-permute-start.6
  91.6 35.9 %all-gather.4.cloned.1.call-done = f32[16,8,32,128]{3,2,1,0:T(8,128)} async-done(((f32[2,8,32,128]{3,2,1,0:T(8,128)}), f32[16,8,32,128]{3,2,1,0:T(8,128)}) %all-gather.4.cloned.1.call-update) | async-done | bytes 2097168 | tf_op jit(solution)/shard_map/all_gather | solution.py:168
  127.5 1.8 %reduce_sum.9 = f32[2,8,32,128]{3,2,1,0:T(8,128)S(1)} reduce(f32[8,2,8,32,128]{4,3,2,1,0:T(8,128)} %bitcast.243, f32[]{:T(128)} %constant.660.clone.1), dimensions={0}, to_apply=%region_2.3 | reduce | flops 458752 | bytes 2359300 | tf_op jit(solution)/shard_map/reduce_sum | solution.py:168
  129.4 0.2 select_select_fusion.3
  129.6 0.8 pad_maximum_fusion
  130.4 3.5 %all-to-all-start.1 = ((f32[4,8,32,128]{3,1,2,0:T(8,128)}), f32[4,8,32,128]{3,1,2,0:T(8,128)S(1)}, u32[]{:S(2)}, u32[]{:S(2)}) async-start(f32[4,8,32,128]{3,1,2,0:T(8,128)} %pad_maximum_fusion), calls=%async_computation.1 | async-start | bytes 1048576 | tf_op jit(solution)/shard_map/all_to_all | solution.py:169
  133.9 1.3 collective-permute-start.7
  135.2 5.4 %collective-permute-done.7 = f32[8,8,128]{2,0,1:T(8,128)S(1)} collective-permute-done((f32[8,8,128]{2,0,1:T(8,128)S(1)}, f32[8,8,128]{2,0,1:T(8,128)S(1)}, u32[]{:S(2)}, u32[]{:S(2)}) %collective-permute-start.7) | collective-permute-done | bytes 32800 | tf_op jit(solution)/shard_map/ppermute | solution.py:15
  140.6 2.0 %all-to-all-done.1 = f32[4,8,32,128]{3,1,2,0:T(8,128)S(1)} async-done(((f32[4,8,32,128]{3,1,2,0:T(8,128)}), f32[4,8,32,128]{3,1,2,0:T(8,128)S(1)}, u32[]{:S(2)}, u32[]{:S(2)}) %all-to-all-start.1) | async-done | bytes 524320 | tf_op jit(solution)/shard_map/all_to_all | solution.py:169
  142.9 0.7 copy.260
  (100 shorter events, 1.5 us)
Async XLA Ops:
  6.5 66.2 %copy-start = (bf16[1,1,2,576,576]{4,3,2,1,0:T(8,128)(2,1)S(1)}, bf16[1,1,2,576,576]{4,3,2,1,0:T(8,128)(2,1)}, u32[]{:S(2)}) copy-start(bf16[1,1,2,576,576]{4,3,2,1,0:T(8,128)(2,1)} %param.51) | copy-start | bytes 3981316
  6.5 42.6 %copy-start.1 = (s32[4,4,3]{1,0,2:T(4,128)S(1)}, s32[4,4,3]{1,0,2:T(4,128)}, u32[]{:S(2)}) copy-start(s32[4,4,3]{1,0,2:T(4,128)} %param.53) | copy-start | bytes 580
  7.5 56.0 %collective-permute-start.1 = (bf16[8,8,128]{2,0,1:T(8,128)(2,1)S(1)}, bf16[8,8,128]{2,0,1:T(8,128)(2,1)S(1)}, u32[]{:S(2)}, u32[]{:S(2)}) collective-permute-start(bf16[8,8,128]{2,0,1:T(8,128)(2,1)S(1)} %get-tuple-element.303), channel_id=1, source_target_pairs={{4,0},{5,1},{6,2},{7,3},{12,8},{13,9},{14,10},{15,11},{20,16},{21,... | collective-permute-start | bytes 49160 | tf_op jit(solution)/shard_map/ppermute | solution.py:15
  8.8 54.7 %collective-permute-start = (bf16[8,8,128]{2,0,1:T(8,128)(2,1)S(1)}, bf16[8,8,128]{2,0,1:T(8,128)(2,1)S(1)}, u32[]{:S(2)}, u32[]{:S(2)}) collective-permute-start(bf16[8,8,128]{2,0,1:T(8,128)(2,1)S(1)} %get-tuple-element.302), channel_id=1, source_target_pairs={{0,4},{1,5},{2,6},{3,7},{8,12},{9,13},{10,14},{11,15},{16,20},{17,... | collective-permute-start | bytes 49160 | tf_op jit(solution)/shard_map/ppermute | solution.py:15
  49.1 15.7 %copy-start.3 = (s32[5]{0:T(128)S(1)}, s32[5]{0:T(128)}, u32[]{:S(2)}) copy-start(s32[5]{0:T(128)} %constant.662.clone.1) | copy-start | bytes 64
  53.9 18.1 %all-to-all-start = ((bf16[4,8,32,128]{3,1,2,0:T(8,128)(2,1)}), bf16[4,8,32,128]{3,1,2,0:T(8,128)(2,1)S(1)}, u32[]{:S(2)}, u32[]{:S(2)}) async-start(bf16[4,8,32,128]{3,1,2,0:T(8,128)(2,1)} %pad_maximum_fusion.1), calls=%async_computation | async-start | bytes 524288 | tf_op jit(solution)/shard_map/all_to_all | solution.py:163
  57.6 70.0 %all-gather.4.cloned.1.call-start = ((), (), s32[]{:S(2)}) async-start(), calls=%async_computation.2 | async-start | bytes 2359296 | tf_op jit(solution)/shard_map/all_gather | solution.py:168
  63.5 6.5 %collective-permute-start.3 = (bf16[32,8,128]{2,1,0:T(8,128)(2,1)S(1)}, bf16[32,8,128]{2,1,0:T(8,128)(2,1)S(1)}, u32[]{:S(2)}, u32[]{:S(2)}) collective-permute-start(bf16[32,8,128]{2,1,0:T(8,128)(2,1)S(1)} %pad_maximum_fusion.4), channel_id=1, source_target_pairs={{1,0},{2,1},{3,2},{4,3},{5,4},{6,5},{7,6},{9,8},{10,9},{11,10},{12... | collective-permute-start | bytes 196616 | tf_op jit(solution)/shard_map/ppermute | solution.py:15
  65.5 6.4 %collective-permute-start.2 = (bf16[32,8,128]{2,1,0:T(8,128)(2,1)S(1)}, bf16[32,8,128]{2,1,0:T(8,128)(2,1)S(1)}, u32[]{:S(2)}, u32[]{:S(2)}) collective-permute-start(bf16[32,8,128]{2,1,0:T(8,128)(2,1)S(1)} %pad_maximum_fusion.4), channel_id=1, source_target_pairs={{0,1},{1,2},{2,3},{3,4},{4,5},{5,6},{6,7},{8,9},{9,10},{10,11},{11... | collective-permute-start | bytes 196616 | tf_op jit(solution)/shard_map/ppermute | solution.py:15
  72.1 0.7 copy-start.2
  78.0 6.8 %collective-permute-start.4 = (f32[32,8,128]{2,1,0:T(8,128)S(1)}, f32[32,8,128]{2,1,0:T(8,128)S(1)}, u32[]{:S(2)}, u32[]{:S(2)}) collective-permute-start(f32[32,8,128]{2,1,0:T(8,128)S(1)} %get-tuple-element.288), channel_id=1, source_target_pairs={{0,1},{1,2},{2,3},{3,4},{4,5},{5,6},{6,7},{8,9},{9,10},{10,11},{11... | collective-permute-start | bytes 393224 | tf_op jit(solution)/shard_map/ppermute | solution.py:15
  82.3 7.9 %collective-permute-start.5 = (f32[32,8,128]{2,1,0:T(8,128)S(1)}, f32[32,8,128]{2,1,0:T(8,128)S(1)}, u32[]{:S(2)}, u32[]{:S(2)}) collective-permute-start(f32[32,8,128]{2,1,0:T(8,128)S(1)} %get-tuple-element.287), channel_id=1, source_target_pairs={{1,0},{2,1},{3,2},{4,3},{5,4},{6,5},{7,6},{9,8},{10,9},{11,10},{12... | collective-permute-start | bytes 393224 | tf_op jit(solution)/shard_map/ppermute | solution.py:15
  90.3 43.5 %collective-permute-start.6 = (f32[8,8,128]{2,0,1:T(8,128)S(1)}, f32[8,8,128]{2,0,1:T(8,128)S(1)}, u32[]{:S(2)}, u32[]{:S(2)}) collective-permute-start(f32[8,8,128]{2,0,1:T(8,128)S(1)} %slice.940), channel_id=1, source_target_pairs={{0,4},{1,5},{2,6},{3,7},{8,12},{9,13},{10,14},{11,15},{16,20},{17,... | collective-permute-start | bytes 98312 | tf_op jit(solution)/shard_map/ppermute | solution.py:15
  130.4 12.3 %all-to-all-start.1 = ((f32[4,8,32,128]{3,1,2,0:T(8,128)}), f32[4,8,32,128]{3,1,2,0:T(8,128)S(1)}, u32[]{:S(2)}, u32[]{:S(2)}) async-start(f32[4,8,32,128]{3,1,2,0:T(8,128)} %pad_maximum_fusion), calls=%async_computation.1 | async-start | bytes 1048576 | tf_op jit(solution)/shard_map/all_to_all | solution.py:169
  133.9 6.7 %collective-permute-start.7 = (f32[8,8,128]{2,0,1:T(8,128)S(1)}, f32[8,8,128]{2,0,1:T(8,128)S(1)}, u32[]{:S(2)}, u32[]{:S(2)}) collective-permute-start(f32[8,8,128]{2,0,1:T(8,128)S(1)} %get-tuple-element.297), channel_id=1, source_target_pairs={{4,0},{5,1},{6,2},{7,3},{12,8},{13,9},{14,10},{15,11},{20,16},{21,... | collective-permute-start | bytes 98312 | tf_op jit(solution)/shard_map/ppermute | solution.py:15
Sparse Core Ops, SparseCore 0:
  78.2 49.3 all-gather.3
